TPU v7x, 32 devices: a whole 2x2x4 slice. The times are simulated.
32 devices in a mesh: rep: 2 (over core), row: 8 (over z, x), col: 2 (over y).
Axes of the slice: x: 2, y: 2, z: 4, core: 2. Of those that a mesh axis runs over, the one named last changes fastest.
Arguments:
- sources: float32 [2, 384, 384, 384], P('rep', 'col', 'row'), may hold values from -6 to 6
Outputs:
- potential: float32 [384, 384, 384], P(('rep', 'col'), 'row')
All inputs are finite; a program needn't handle non-finite values.
Results may differ from a plain program's by a relative error of at most 0.000096.
Values sent between devices are 32-bit elements; how exact they have to be, the bound alone decides.
A program may use at most 128 MiB of HBM per device.

v0:
```python
import math

import jax
import jax.numpy as jnp
from jax import lax
from jax.sharding import PartitionSpec as P

NA = 384
NB = 384
NC = 384


highest = lax.Precision.HIGHEST


def wave_tables(freq_index, position, length):
    turns = freq_index[:, None] * position[None, :] % length
    angle = turns.astype(jnp.float32) * (2.0 * math.pi / length)
    return (jnp.cos(angle), jnp.sin(angle))


def matmul_high(first_matrix, second_matrix):
    return jnp.dot(
        first_matrix, second_matrix, precision=highest, preferred_element_type=jnp.float32
    )


def leading_contract(first_matrix, second_matrix):
    return lax.dot_general(
        first_matrix,
        second_matrix,
        (((0,), (0,)), ((), ())),
        precision=highest,
        preferred_element_type=jnp.float32,
    )


def trailing_contract(first_matrix, second_matrix):
    return lax.dot_general(
        first_matrix,
        second_matrix,
        (((1,), (1,)), ((), ())),
        precision=highest,
        preferred_element_type=jnp.float32,
    )


def table_against_rows(table, flat_rows):
    return lax.dot_general(
        table,
        flat_rows,
        (((0,), (1,)), ((), ())),
        precision=highest,
        preferred_element_type=jnp.float32,
    )


def laplace_eigen(wave_index, length):
    sines = jnp.sin(wave_index.astype(jnp.float32) * (math.pi / length))
    return 4.0 * sines * sines


def mirror_modes(values, axis_number):
    return jnp.roll(jnp.flip(values, axis_number), 1, axis_number)


def body(sources):
    partial_value = sources[0]
    density = lax.psum_scatter(partial_value, "rep", scatter_dimension=0, tiled=True)
    slab_rows, line_rows, length_c = density.shape
    rep_count = lax.axis_size("rep")
    col_count = lax.axis_size("col")
    third_len = NC // 2
    freq_block = third_len // (rep_count * col_count)
    half_first = NA // 2
    modes_first = jnp.arange(NA, dtype=jnp.int32)
    modes_second = jnp.arange(NB, dtype=jnp.int32)
    modes_third = jnp.arange(NC, dtype=jnp.int32)
    modes_spec = jnp.arange(third_len, dtype=jnp.int32)
    parity = (1 - 2 * (modes_third % 2)).astype(jnp.float32)
    owner_zero = (lax.axis_index("rep") == 0) & (lax.axis_index("col") == 0)
    flat_density = density.reshape(slab_rows * line_rows, NC)
    cos_spec, sin_spec = wave_tables(modes_spec, modes_third, NC)
    sin_spec = jnp.where(modes_spec[:, None] == 0, -parity[None, :], sin_spec)
    real_third = trailing_contract(flat_density, cos_spec).reshape(slab_rows, line_rows, third_len)
    imag_third = (-trailing_contract(flat_density, sin_spec)).reshape(
        slab_rows, line_rows, third_len
    )
    group_first = modes_first // slab_rows
    first_index = (
        group_first % col_count * (rep_count * slab_rows)
        + group_first // col_count * slab_rows
        + modes_first % slab_rows
    )
    cos_first, sin_first = wave_tables(first_index, modes_first, NA)
    real_in = lax.all_to_all(real_third, ("rep", "col"), split_axis=2, concat_axis=0, tiled=True)
    imag_in = lax.all_to_all(imag_third, ("rep", "col"), split_axis=2, concat_axis=0, tiled=True)
    count = real_in.shape[1]
    flat_real = real_in.reshape(NA, count * freq_block)
    flat_imag = imag_in.reshape(NA, count * freq_block)
    real_out = leading_contract(flat_real, cos_first) + leading_contract(flat_imag, sin_first)
    imag_out = leading_contract(flat_imag, cos_first) - leading_contract(flat_real, sin_first)
    real_first = real_out.reshape(count, freq_block, NA)
    imag_first = imag_out.reshape(count, freq_block, NA)
    packed_r = real_first[:, 0, :]
    packed_i = imag_first[:, 0, :]
    mirror_r = mirror_modes(packed_r, 1)
    mirror_i = mirror_modes(packed_i, 1)
    zero_r = 0.5 * (packed_r + mirror_r)
    zero_i = 0.5 * (packed_i - mirror_i)
    top_r = 0.5 * (packed_i + mirror_i)
    top_i = -0.5 * (packed_r - mirror_r)
    edge_modes = ((modes_first == 0) | (modes_first == half_first))[None, :]
    lower_modes = (modes_first <= half_first)[None, :]
    new_r = jnp.where(lower_modes, zero_r, top_r)
    new_i = jnp.where(edge_modes, top_r, jnp.where(lower_modes, zero_i, top_i))
    real_first = real_first.at[:, 0, :].set(jnp.where(owner_zero, new_r, packed_r))
    imag_first = imag_first.at[:, 0, :].set(jnp.where(owner_zero, new_i, packed_i))
    cos_second, sin_second = wave_tables(modes_second, modes_second, NB)
    real_in = lax.all_to_all(real_first, "row", split_axis=2, concat_axis=0, tiled=True)
    imag_in = lax.all_to_all(imag_first, "row", split_axis=2, concat_axis=0, tiled=True)
    count = real_in.shape[1]
    tail = real_in.shape[2]
    flat_real = real_in.reshape(NB, count * tail)
    flat_imag = imag_in.reshape(NB, count * tail)
    real_out = matmul_high(cos_second, flat_real) + matmul_high(sin_second, flat_imag)
    imag_out = matmul_high(cos_second, flat_imag) - matmul_high(sin_second, flat_real)
    real_second = real_out.reshape(NB, count, tail)
    imag_second = imag_out.reshape(NB, count, tail)
    freq_rows = real_second.shape[2]
    first_freqs = lax.axis_index("row") * freq_rows + jnp.arange(freq_rows, dtype=jnp.int32)
    third_freqs = (
        lax.axis_index("rep") * col_count + lax.axis_index("col")
    ) * freq_block + jnp.arange(freq_block, dtype=jnp.int32)
    scale_all = 1.0 / (NA * NB * NC)
    eigen_second = laplace_eigen(modes_second, NB)
    eigen_first = laplace_eigen(first_freqs, NA)
    total = (
        eigen_second[:, None, None]
        + laplace_eigen(third_freqs, NC)[None, :, None]
        + eigen_first[None, None, :]
        + 0.001
    )
    green = 1.0 / total * scale_all
    filt_real = real_second * green
    filt_imag = imag_second * green
    wave_r = real_second[:, 0, :]
    wave_i = imag_second[:, 0, :]
    green_zero = green[:, 0, :]
    green_top = 1.0 / (eigen_second[:, None] + 4.0 + eigen_first[None, :] + 0.001) * scale_all
    mean_green = 0.5 * (green_zero + green_top)
    diff_green = 0.5 * (green_zero - green_top)
    mixed_r = mean_green * wave_r + diff_green * mirror_modes(wave_r, 0)
    mixed_i = mean_green * wave_i - diff_green * mirror_modes(wave_i, 0)
    lower_freqs = ((first_freqs > 0) & (first_freqs < half_first))[None, :]
    upper_freqs = (first_freqs > half_first)[None, :]
    slot_r = jnp.where(
        lower_freqs, green_zero * wave_r, jnp.where(upper_freqs, green_top * wave_r, mixed_r)
    )
    slot_i = jnp.where(
        lower_freqs, green_zero * wave_i, jnp.where(upper_freqs, green_top * wave_i, mixed_i)
    )
    filt_real = filt_real.at[:, 0, :].set(jnp.where(owner_zero, slot_r, filt_real[:, 0, :]))
    filt_imag = filt_imag.at[:, 0, :].set(jnp.where(owner_zero, slot_i, filt_imag[:, 0, :]))
    flat_real = filt_real.reshape(NB, freq_block * freq_rows)
    flat_imag = filt_imag.reshape(NB, freq_block * freq_rows)
    real_back = (matmul_high(cos_second, flat_real) - matmul_high(sin_second, flat_imag)).reshape(
        NB, freq_block, freq_rows
    )
    imag_back = (matmul_high(cos_second, flat_imag) + matmul_high(sin_second, flat_real)).reshape(
        NB, freq_block, freq_rows
    )
    cos_inverse, sin_inverse = wave_tables(modes_first, modes_first, NA)
    real_in = lax.all_to_all(real_back, "row", split_axis=0, concat_axis=2, tiled=True)
    imag_in = lax.all_to_all(imag_back, "row", split_axis=0, concat_axis=2, tiled=True)
    b_count = real_in.shape[0]
    count = real_in.shape[1]
    flat_real_in = real_in.reshape(b_count * count, NA)
    flat_imag_in = imag_in.reshape(b_count * count, NA)
    real_out = table_against_rows(cos_inverse, flat_real_in) - table_against_rows(
        sin_inverse, flat_imag_in
    )
    imag_out = table_against_rows(cos_inverse, flat_imag_in) + table_against_rows(
        sin_inverse, flat_real_in
    )
    real_lines = real_out.reshape(NA, b_count, count)
    imag_lines = imag_out.reshape(NA, b_count, count)
    field_r = real_lines[:, :, 0]
    field_i = imag_lines[:, :, 0]
    spec_r = (matmul_high(cos_inverse, field_r) + matmul_high(sin_inverse, field_i)) * (1.0 / NA)
    spec_i = (matmul_high(cos_inverse, field_i) - matmul_high(sin_inverse, field_r)) * (1.0 / NA)
    mirror_r = mirror_modes(spec_r, 0)
    mirror_i = mirror_modes(spec_i, 0)
    lower_lines = ((modes_first > 0) & (modes_first < half_first))[:, None]
    upper_lines = (modes_first > half_first)[:, None]
    joined_r = jnp.where(
        lower_lines, spec_r + mirror_i, jnp.where(upper_lines, mirror_r - spec_i, spec_r)
    )
    joined_i = jnp.where(
        lower_lines, spec_i + mirror_r, jnp.where(upper_lines, spec_r - mirror_i, spec_i)
    )
    rebuilt_r = matmul_high(cos_inverse, joined_r) - matmul_high(sin_inverse, joined_i)
    rebuilt_i = matmul_high(cos_inverse, joined_i) + matmul_high(sin_inverse, joined_r)
    real_lines = real_lines.at[:, :, 0].set(jnp.where(owner_zero, rebuilt_r, field_r))
    imag_lines = imag_lines.at[:, :, 0].set(jnp.where(owner_zero, rebuilt_i, field_i))
    cos_final, sin_final = wave_tables(modes_spec, modes_third, NC)
    weight = jnp.where(modes_spec == 0, 1.0, 2.0).astype(jnp.float32)[:, None]
    cos_final = weight * cos_final
    sin_final = jnp.where(modes_spec[:, None] == 0, -parity[None, :], 2.0 * sin_final)
    real_in = lax.all_to_all(real_lines, ("rep", "col"), split_axis=0, concat_axis=2, tiled=True)
    imag_in = lax.all_to_all(imag_lines, ("rep", "col"), split_axis=0, concat_axis=2, tiled=True)
    a_count = real_in.shape[0]
    count = real_in.shape[1]
    spec_len = real_in.shape[2]
    flat_real_in = real_in.reshape(a_count * count, spec_len)
    flat_imag_in = imag_in.reshape(a_count * count, spec_len)
    result = matmul_high(flat_real_in, cos_final) - matmul_high(flat_imag_in, sin_final)
    return result.reshape(a_count, count, NC)


def solution(mesh):
    in_specs = (P("rep", "col", "row", None),)
    out_specs = P(("rep", "col"), "row", None)
    return jax.shard_map(body, mesh=mesh, in_specs=in_specs, out_specs=out_specs, check_vma=False)
```

profile of v0, /device:TPU:0, one launch (start us, length us, event | category | flops | bytes accessed | tf_op | source)
XLA Modules:
  0.0 1180.1 jit_solution(17510025944328958917)
XLA Ops:
  7.3 29.3 %reduce-scatter.2.cloned.1.call-done = f32[96,48,384]{2,1,0:T(8,128)} async-done(((f32[192,48,384]{2,1,0:T(8,128)}), f32[96,48,384]{2,1,0:T(8,128)}) %reduce-scatter.2.cloned.1.call-update) | async-done | bytes 7077904 | tf_op jit(solution)/shard_map/reduce_scatter | solution.py:69
  36.6 12.2 %convolution_bitcast_fusion = f32[4608,192]{0,1:T(8,128)S(1)} fusion(f32[4608,384]{1,0:T(8,128)} %bitcast.153), kind=kOutput, calls=%fused_computation.5 | convolution fusion | flops 4077527040 | bytes 10616832 | tf_op jit(solution)/shard_map/dot_general | solution.py:39
  65.8 12.3 %fusion = f32[4608,192]{0,1:T(8,128)S(1)} fusion(f32[4608,384]{1,0:T(8,128)} %bitcast.154, f32[384]{0:T(512)S(1)} %fusion.186, pred[192]{0:T(512)(128)(4,1)S(1)} %iota_compare_fusion.6), kind=kOutput, calls=%fused_computation.4 | convolution fusion | flops 4078485504 | bytes 10618560 | tf_op jit(solution)/shard_map/dot_general | solution.py:39
  88.6 29.8 %all-to-all-done = f32[96,48,192]{0,1,2:T(8,128)} async-done(((f32[96,48,192]{0,1,2:T(8,128)}), f32[96,48,192]{0,1,2:T(8,128)}, u32[]{:S(2)}, u32[]{:S(2)}) %all-to-all-start) | async-done | bytes 3538976 | tf_op jit(solution)/shard_map/all_to_all | solution.py:96
  135.9 41.8 %all-to-all-done.1 = f32[96,48,192]{0,1,2:T(8,128)} async-done(((f32[96,48,192]{0,1,2:T(8,128)}), f32[96,48,192]{0,1,2:T(8,128)}, u32[]{:S(2)}, u32[]{:S(2)}) %all-to-all-start.1) | async-done | bytes 3538976 | tf_op jit(solution)/shard_map/all_to_all | solution.py:97
  245.4 24.0 %scatter.20 = f32[48,48,384]{1,0,2:T(8,128)} dynamic-update-slice(f32[48,48,384]{1,0,2:T(8,128)} %copy.173, f32[48,1,384]{1,0,2:T(8,128)} %copy.174, s32[]{:T(128)} %constant.236.clone.1, s32[]{:T(128)} %constant.236.clone.1, s32[]{:T(128)} %constant.236.clone.1) | dynamic-update-slice | bytes 147460 | tf_op jit(solution)/shard_map/scatter | solution.py:117
  269.4 12.1 %reshape.531 = f32[8,1,110592]{2,1,0:T(1,128)} reshape(f32[384,48,48]{2,1,0:T(8,128)} %bitcast.137) | data formatting | bytes 7077888
  300.1 24.0 %scatter.21 = f32[48,48,384]{1,0,2:T(8,128)} dynamic-update-slice(f32[48,48,384]{1,0,2:T(8,128)} %copy.177, f32[48,1,384]{1,0,2:T(8,128)} %copy.178, s32[]{:T(128)} %constant.236.clone.1, s32[]{:T(128)} %constant.236.clone.1, s32[]{:T(128)} %constant.236.clone.1) | dynamic-update-slice | bytes 147460 | tf_op jit(solution)/shard_map/scatter | solution.py:118
  336.1 30.5 %all-to-all-done.2 = f32[8,1,110592]{2,1,0:T(1,128)} async-done(((f32[8,1,110592]{2,1,0:T(1,128)}), f32[8,1,110592]{2,1,0:T(1,128)}, u32[]{:S(2)}, u32[]{:S(2)}) %all-to-all-start.2) | async-done | bytes 3538976 | tf_op jit(solution)/shard_map/all_to_all | solution.py:120
  372.6 37.3 %reduce.13 = f32[8,110592]{1,0:T(8,128)S(1)} reduce(f32[8,1,110592]{2,1,0:T(1,128)} %all-to-all-done.2, f32[]{:T(128)} %broadcast.614), dimensions={1}, to_apply=%all_to_all.94.reduce_sub_computation | reduce | bytes 7077892 | tf_op jit(solution)/shard_map/all_to_all | solution.py:120
  449.7 39.4 %reduce.12 = f32[8,110592]{1,0:T(8,128)} reduce(f32[8,1,110592]{2,1,0:T(1,128)} %all-to-all-done.3, f32[]{:T(128)} %broadcast.614), dimensions={1}, to_apply=%all_to_all.97.reduce_sub_computation | reduce | bytes 7077892 | tf_op jit(solution)/shard_map/all_to_all | solution.py:121
  665.9 36.9 %all-to-all-done.5 = f32[8,1,110592]{2,1,0:T(1,128)} async-done(((f32[8,1,110592]{2,1,0:T(1,128)}), f32[8,1,110592]{2,1,0:T(1,128)}, u32[]{:S(2)}, u32[]{:S(2)}) %all-to-all-start.5) | async-done | bytes 3538976 | tf_op jit(solution)/shard_map/all_to_all | solution.py:175
  707.3 37.4 %reduce.15 = f32[8,110592]{1,0:T(8,128)S(1)} reduce(f32[8,1,110592]{2,1,0:T(1,128)} %all-to-all-done.5, f32[]{:T(128)} %broadcast.614), dimensions={1}, to_apply=%all_to_all.103.reduce_sub_computation | reduce | bytes 7077892 | tf_op jit(solution)/shard_map/all_to_all | solution.py:175
  752.2 12.8 %copy.227 = f32[8,48,48,48]{3,0,2,1:T(8,128)} copy(f32[8,48,48,48]{3,2,1,0:T(8,128)} %bitcast.141) | data formatting | bytes 7077888 | tf_op jit(solution)/shard_map/all_to_all | solution.py:175
  771.8 12.5 %fusion.31 = f32[384,2304]{1,0:T(8,128)} fusion(f32[2304,384]{1,0:T(8,128)S(1)} %reshape.523), kind=kOutput, calls=%fused_computation.46 | convolution fusion | flops 4078190592 | bytes 7077888 | tf_op jit(solution)/shard_map/dot_general | solution.py:49
  785.8 39.8 %reduce.14 = f32[8,110592]{1,0:T(8,128)} reduce(f32[8,1,110592]{2,1,0:T(1,128)} %all-to-all-done.4, f32[]{:T(128)} %broadcast.614), dimensions={1}, to_apply=%all_to_all.100.reduce_sub_computation | reduce | bytes 7077892 | tf_op jit(solution)/shard_map/all_to_all | solution.py:174
  835.1 12.8 %copy.228 = f32[8,48,48,48]{3,0,2,1:T(8,128)} copy(f32[8,48,48,48]{3,2,1,0:T(8,128)} %bitcast.143) | data formatting | bytes 7077888 | tf_op jit(solution)/shard_map/all_to_all | solution.py:174
  856.3 14.6 %fusion.37 = f32[384,2304]{1,0:T(8,128)} fusion(f32[2304,384]{1,0:T(8,128)} %reshape.521), kind=kOutput, calls=%fused_computation.49 | convolution fusion | flops 4078190592 | bytes 7077888 | tf_op jit(solution)/shard_map/dot_general | solution.py:49
  870.9 13.1 %convolution_add_fusion = f32[384,2304]{1,0:T(8,128)} fusion(f32[384,2304]{1,0:T(8,128)S(1)} %copy-done.9, f32[2304,384]{1,0:T(8,128)S(1)} %copy-done.3), kind=kOutput, calls=%fused_computation.6 | convolution fusion | flops 4079075328 | bytes 10616832 | tf_op jit(solution)/shard_map/dot_general | solution.py:49
  890.9 15.7 %convolution_subtract_fusion.1 = f32[384,2304]{1,0:T(8,128)} fusion(f32[384,2304]{1,0:T(8,128)} %fusion.37, f32[2304,384]{1,0:T(8,128)S(1)} %reshape.523), kind=kOutput, calls=%fused_computation.7 | convolution fusion | flops 4079075328 | bytes 10616832 | tf_op jit(solution)/shard_map/dot_general | solution.py:49
  999.4 12.6 %all-to-all-done.7 = f32[4,1,221184]{2,1,0:T(1,128)} async-done(((f32[4,1,221184]{2,1,0:T(1,128)}), f32[4,1,221184]{2,1,0:T(1,128)}, u32[]{:S(2)}, u32[]{:S(2)}) %all-to-all-start.7) | async-done | bytes 3538976 | tf_op jit(solution)/shard_map/all_to_all | solution.py:211
  1015.9 40.4 %reduce.17 = f32[4,221184]{1,0:T(4,128)} reduce(f32[4,1,221184]{2,1,0:T(1,128)} %all-to-all-done.7, f32[]{:T(128)} %broadcast.614), dimensions={1}, to_apply=%all_to_all.109.reduce_sub_computation | reduce | bytes 7077892 | tf_op jit(solution)/shard_map/all_to_all | solution.py:211
  1088.1 32.6 %reduce.16 = f32[4,221184]{1,0:T(4,128)} reduce(f32[4,1,221184]{2,1,0:T(1,128)S(1)} %all-to-all-done.6, f32[]{:T(128)} %broadcast.614), dimensions={1}, to_apply=%all_to_all.106.reduce_sub_computation | reduce | bytes 7077892 | tf_op jit(solution)/shard_map/all_to_all | solution.py:210
  1160.4 12.6 %convolution_subtract_fusion = f32[4608,384]{1,0:T(8,128)} fusion(f32[4608,384]{1,0:T(8,128)S(1)} %fusion.61, f32[4608,192]{0,1:T(8,128)S(1)} %copy-done.10, f32[384]{0:T(512)S(1)} %copy-done.21, pred[192]{0:T(512)(128)(4,1)S(1)} %copy-done.23), kind=kOutput, calls=%fused_computation.2 | convolution fusion | flops 4079443968 | bytes 17696448 | tf_op jit(solution)/shard_map/dot_general | solution.py:23
  (173 shorter events, 579.3 us)
Async XLA Ops:
  6.5 30.1 %reduce-scatter.2.cloned.1.call-start = ((), (), s32[]{:S(2)}) async-start(), calls=%async_computation.9 | async-start | bytes 21233664 | tf_op jit(solution)/shard_map/reduce_scatter | solution.py:69
  59.3 59.1 %all-to-all-start = ((f32[96,48,192]{0,1,2:T(8,128)}), f32[96,48,192]{0,1,2:T(8,128)}, u32[]{:S(2)}, u32[]{:S(2)}) async-start(f32[96,48,192]{0,1,2:T(8,128)} %copy.162), calls=%async_computation.1 | async-start | bytes 9437184 | tf_op jit(solution)/shard_map/all_to_all | solution.py:96
  118.4 59.3 %all-to-all-start.1 = ((f32[96,48,192]{0,1,2:T(8,128)}), f32[96,48,192]{0,1,2:T(8,128)}, u32[]{:S(2)}, u32[]{:S(2)}) async-start(f32[96,48,192]{0,1,2:T(8,128)} %copy.166), calls=%async_computation.2 | async-start | bytes 9437184 | tf_op jit(solution)/shard_map/all_to_all | solution.py:97
  191.2 8.9 copy-start.1
  218.5 9.9 copy-start.7
  230.5 8.5 copy-start.12
  281.5 6.2 copy-start.6
  281.5 85.1 %all-to-all-start.2 = ((f32[8,1,110592]{2,1,0:T(1,128)}), f32[8,1,110592]{2,1,0:T(1,128)}, u32[]{:S(2)}, u32[]{:S(2)}) async-start(f32[8,1,110592]{2,1,0:T(1,128)} %reshape.531), calls=%async_computation.3 | async-start | bytes 7077888 | tf_op jit(solution)/shard_map/all_to_all | solution.py:120
  366.6 83.1 %all-to-all-start.3 = ((f32[8,1,110592]{2,1,0:T(1,128)}), f32[8,1,110592]{2,1,0:T(1,128)}, u32[]{:S(2)}, u32[]{:S(2)}) async-start(f32[8,1,110592]{2,1,0:T(1,128)} %reshape.533), calls=%async_computation.4 | async-start | bytes 7077888 | tf_op jit(solution)/shard_map/all_to_all | solution.py:121
  517.2 11.9 %copy-start.2 = (f32[384,2304]{1,0:T(8,128)S(1)}, f32[384,2304]{1,0:T(8,128)}, u32[]{:S(2)}) copy-start(f32[384,2304]{1,0:T(8,128)} %reshape.515) | copy-start | bytes 10616836
  517.2 11.9 %copy-start.8 = (f32[384,2304]{1,0:T(8,128)S(1)}, f32[384,2304]{1,0:T(8,128)}, u32[]{:S(2)}) copy-start(f32[384,2304]{1,0:T(8,128)} %fusion.43) | copy-start | bytes 10616836
  561.7 8.3 copy-start.4
  571.0 4.2 copy-start.14
  571.0 4.2 copy-start.15
  576.3 8.2 copy-start
  619.7 83.1 %all-to-all-start.5 = ((f32[8,1,110592]{2,1,0:T(1,128)}), f32[8,1,110592]{2,1,0:T(1,128)}, u32[]{:S(2)}, u32[]{:S(2)}) async-start(f32[8,1,110592]{2,1,0:T(1,128)} %reshape.537), calls=%async_computation.6 | async-start | bytes 7077888 | tf_op jit(solution)/shard_map/all_to_all | solution.py:175
  702.8 83.1 %all-to-all-start.4 = ((f32[8,1,110592]{2,1,0:T(1,128)}), f32[8,1,110592]{2,1,0:T(1,128)}, u32[]{:S(2)}, u32[]{:S(2)}) async-start(f32[8,1,110592]{2,1,0:T(1,128)} %reshape.535), calls=%async_computation.5 | async-start | bytes 7077888 | tf_op jit(solution)/shard_map/all_to_all | solution.py:174
  856.3 14.6 %copy-start.3 = (f32[2304,384]{1,0:T(8,128)S(1)}, f32[2304,384]{1,0:T(8,128)}, u32[]{:S(2)}) copy-start(f32[2304,384]{1,0:T(8,128)} %reshape.521) | copy-start | bytes 10616836
  856.3 14.6 %copy-start.9 = (f32[384,2304]{1,0:T(8,128)S(1)}, f32[384,2304]{1,0:T(8,128)}, u32[]{:S(2)}) copy-start(f32[384,2304]{1,0:T(8,128)} %fusion.31) | copy-start | bytes 10616836
  965.6 46.3 %all-to-all-start.7 = ((f32[4,1,221184]{2,1,0:T(1,128)}), f32[4,1,221184]{2,1,0:T(1,128)}, u32[]{:S(2)}, u32[]{:S(2)}) async-start(f32[4,1,221184]{2,1,0:T(1,128)} %reshape.541), calls=%async_computation.8 | async-start | bytes 7077888 | tf_op jit(solution)/shard_map/all_to_all | solution.py:211
  1012.0 76.1 %all-to-all-start.6 = ((f32[4,1,221184]{2,1,0:T(1,128)}), f32[4,1,221184]{2,1,0:T(1,128)S(1)}, u32[]{:S(2)}, u32[]{:S(2)}) async-start(f32[4,1,221184]{2,1,0:T(1,128)} %reshape.539), calls=%async_computation.7 | async-start | bytes 7077888 | tf_op jit(solution)/shard_map/all_to_all | solution.py:210
  1151.4 8.9 copy-start.10
  1151.4 8.9 copy-start.21
  1151.4 8.9 copy-start.23
  (9 other events, 15.1 us)
Sparse Core Ops, SparseCore 0:
  9.6 26.9 reduce-scatter.1
where the time goes:
time: 1190 us; the launch traced here: 1180 us
  local copies, waits for them, and re-layouts  451 us (38%)
  matrix products  251 us (21%)
  other arithmetic  237 us (20%)
  waiting for transfers between devices  188 us (16%)
  starting transfers between devices  39.5 us (3%)
  between operations  14.3 us (1%)
    unnamed x66, local copies, waits for them, and re-layouts  135 us
    dot_general x18, matrix products, matmul_high(): jnp.dot(first_matrix, second_matrix, precision=highest, preferred_element...  134 us
    dot_general x4, matrix products, table_against_rows(): lax.dot_general(table, flat_rows, (((0,), (1,)), ((), ())), precision=hig...  55.9 us
    all_to_all x1, waiting for transfers between devices, body(): lax.all_to_all(imag_third, ('rep', 'col'), split_axis=2, concat_axis=0, t...  41.8 us
    all_to_all x1, other arithmetic, body(): lax.all_to_all(imag_lines, ('rep', 'col'), split_axis=0, concat_axis=2, t...  40.4 us
    all_to_all x1, other arithmetic, body(): lax.all_to_all(real_back, 'row', split_axis=0, concat_axis=2, tiled=True)  39.8 us
    all_to_all x1, other arithmetic, body(): lax.all_to_all(imag_first, 'row', split_axis=2, concat_axis=0, tiled=True)  39.4 us
    all_to_all x1, other arithmetic, body(): lax.all_to_all(imag_back, 'row', split_axis=0, concat_axis=2, tiled=True)  37.4 us
  transfers between devices with their start and end apart: 9, of which 8 were waited for; matrix products, arithmetic and copies ran while one was open for 32% of the time, Pallas kernels for 0%

commit v1 on v0

--- a/solution.py
+++ b/solution.py
@@ -1,8 +1,12 @@
+import functools
 import math
 
 import jax
 import jax.numpy as jnp
+import numpy as np
 from jax import lax
+from jax.experimental import pallas as pl
+from jax.experimental.pallas import tpu as pltpu
 from jax.sharding import PartitionSpec as P
 
 NA = 384
@@ -218,7 +222,203 @@
     return result.reshape(a_count, count, NC)
 
 
+def slab_tables(length):
+    turns = np.outer(np.arange(length), np.arange(length)) % length
+    angle = turns * (2.0 * np.pi / length)
+    table = np.cos(angle) + np.sin(angle)
+    high = table.astype(jnp.bfloat16)
+    low = (table - high.astype(np.float64)).astype(jnp.bfloat16)
+    return jnp.asarray(high), jnp.asarray(low)
+
+
+def eigen_values(length):
+    sines = np.sin(np.arange(length) * (np.pi / length))
+    return (4.0 * sines * sines).astype(np.float32)
+
+
+def halves(value):
+    high = value.astype(jnp.bfloat16)
+    low = (value - high.astype(jnp.float32)).astype(jnp.bfloat16)
+    return high, low
+
+
+def dot_f32(left, right):
+    return jnp.dot(left, right, preferred_element_type=jnp.float32)
+
+
+def times_table(value, high, low):
+    top, rest = halves(value)
+    return dot_f32(top, high) + dot_f32(top, low) + dot_f32(rest, high)
+
+
+def table_times(high, low, value):
+    top, rest = halves(value)
+    return dot_f32(high, top) + dot_f32(low, top) + dot_f32(high, rest)
+
+
+def decay_of(shift):
+    root = jnp.sqrt(shift * (shift + 4.0))
+    return 2.0 / (2.0 + shift + root), root
+
+
+def forward_kernel(ah, al, ch, cl, eig_a, eig_c, x_ref, z_ref, up_ref, down_ref, rho, power):
+    step = pl.program_id(0)
+    lines = times_table(x_ref[0], ch[...], cl[...])
+    modes = table_times(ah[...], al[...], lines)
+    z_ref[0] = modes
+
+    @pl.when(step == 0)
+    def _():
+        rho[...] = decay_of(eig_a[...] + eig_c[...] + 0.001)[0]
+        power[...] = rho[...]
+        up_ref[...] = modes
+        down_ref[...] = modes
+
+    @pl.when(step > 0)
+    def _():
+        up_ref[...] = modes + rho[...] * up_ref[...]
+        down_ref[...] = down_ref[...] + power[...] * modes
+        power[...] = power[...] * rho[...]
+
+
+def backward_kernel(scale, ah, al, ch, cl, eig_a, eig_c, z_ref, carry, out_ref, rho, gain, run, back):
+    step = pl.program_id(0)
+    count = z_ref.shape[0]
+
+    @pl.when(step == 0)
+    def _():
+        decay, root = decay_of(eig_a[...] + eig_c[...] + 0.001)
+        rho[...] = decay
+        gain[...] = scale / root
+        run[...] = carry[0]
+        back[count - 1] = decay * carry[1]
+
+        def down(t, _):
+            here = count - 2 - t
+            back[here] = rho[...] * (z_ref[here + 1] + back[here + 1])
+            return 0
+
+        lax.fori_loop(0, count - 1, down, 0)
+
+    run[...] = z_ref[step] + rho[...] * run[...]
+    field = gain[...] * (run[...] + back[step])
+    lines = table_times(ah[...], al[...], field)
+    out_ref[0] = times_table(lines, ch[...], cl[...])
+
+
+def whole(shape):
+    return pl.BlockSpec(shape, lambda t: (0,) * len(shape))
+
+
+def forward_call(x, tables):
+    count, rows, cols = x.shape
+    plane = jax.ShapeDtypeStruct((rows, cols), jnp.float32)
+    return pl.pallas_call(
+        forward_kernel,
+        grid=(count,),
+        in_specs=[whole(t.shape) for t in tables]
+        + [pl.BlockSpec((1, rows, cols), lambda t: (t, 0, 0))],
+        out_specs=[
+            pl.BlockSpec((1, rows, cols), lambda t: (t, 0, 0)),
+            whole((rows, cols)),
+            whole((rows, cols)),
+        ],
+        out_shape=[jax.ShapeDtypeStruct(x.shape, jnp.float32), plane, plane],
+        scratch_shapes=[pltpu.VMEM((rows, cols), jnp.float32)] * 2,
+    )(*tables, x)
+
+
+def backward_call(z, carry, tables, scale):
+    count, rows, cols = z.shape
+    return pl.pallas_call(
+        functools.partial(backward_kernel, scale),
+        grid=(count,),
+        in_specs=[whole(t.shape) for t in tables] + [whole(z.shape), whole(carry.shape)],
+        out_specs=pl.BlockSpec((1, rows, cols), lambda t: (t, 0, 0)),
+        out_shape=jax.ShapeDtypeStruct(z.shape, jnp.float32),
+        scratch_shapes=[pltpu.VMEM((rows, cols), jnp.float32)] * 3
+        + [pltpu.VMEM(z.shape, jnp.float32)],
+        compiler_params=pltpu.CompilerParams(vmem_limit_bytes=50 * 1024 * 1024),
+    )(*tables, z, carry)
+
+
+def carries(up, down, count, eig_a, eig_c):
+    rows, cols = up.shape
+    rep_count = lax.axis_size("rep")
+    col_count = lax.axis_size("col")
+    row_count = lax.axis_size("row")
+    group = rep_count * col_count
+    part = rows // group
+    member = lax.axis_index("rep") * col_count + lax.axis_index("col")
+    row = lax.axis_index("row")
+    ends = jnp.stack([up, down]).reshape(2, group, part, cols)
+    ends = lax.all_to_all(ends, ("rep", "col"), split_axis=1, concat_axis=1)
+    eig_part = lax.dynamic_slice_in_dim(jnp.asarray(eig_a), member * part, part, 0)
+    rho, _ = decay_of(eig_part[:, None] + jnp.asarray(eig_c)[None, :] + 0.001)
+    block = lax.integer_pow(rho, count)
+    wide = lax.integer_pow(block, group)
+    total_up = ends[0, 0]
+    total_down = ends[1, group - 1]
+    for j in range(1, group):
+        total_up = ends[0, j] + block * total_up
+        total_down = ends[1, group - 1 - j] + block * total_down
+    every = lax.all_gather(jnp.stack([total_up, total_down]), "row", axis=0)
+
+    def pick(offset, side):
+        return lax.dynamic_index_in_dim(every, (row + offset) % row_count, 0, False)[side]
+
+    into_up = pick(0, 0)
+    into_down = pick(0, 1)
+    for m in range(row_count - 1, 0, -1):
+        into_up = pick(row_count - m, 0) + wide * into_up
+        into_down = pick(m, 1) + wide * into_down
+    closing = 1.0 / (1.0 - lax.integer_pow(wide, row_count))
+    ups = [into_up * closing]
+    downs = [into_down * closing]
+    for j in range(group - 1):
+        ups.append(ends[0, j] + block * ups[-1])
+        downs.append(ends[1, group - 1 - j] + block * downs[-1])
+    back = jnp.stack([jnp.stack(ups), jnp.stack(downs[::-1])])
+    back = lax.all_to_all(back, ("rep", "col"), split_axis=1, concat_axis=1)
+    return back.reshape(2, rows, cols)
+
+
+def line_body(sources):
+    partial_value = sources[0]
+    rep_count = lax.axis_size("rep")
+    col_count = lax.axis_size("col")
+    slab, width, length_c = partial_value.shape
+    length_a = slab * col_count
+    length_b = width * lax.axis_size("row")
+    half = width // rep_count
+    rep = lax.axis_index("rep")
+    part = half // col_count
+    by_line = partial_value.transpose(1, 0, 2)
+    mine = lax.psum_scatter(by_line, "rep", scatter_dimension=0, tiled=True)
+    lines = lax.all_to_all(mine, "col", split_axis=0, concat_axis=1, tiled=True)
+    high_a, low_a = slab_tables(length_a)
+    high_c, low_c = slab_tables(length_c)
+    eig_a = eigen_values(length_a)
+    eig_c = eigen_values(length_c)
+    tables = (
+        high_a,
+        low_a,
+        high_c,
+        low_c,
+        jnp.asarray(eig_a)[:, None],
+        jnp.asarray(eig_c)[None, :],
+    )
+    modes, up, down = forward_call(lines, tables)
+    carry = carries(up, down, part, eig_a, eig_c)
+    field = backward_call(modes, carry, tables, 1.0 / (length_a * length_c))
+    result = lax.all_to_all(field, ("rep", "col"), split_axis=1, concat_axis=0, tiled=True)
+    return result.transpose(1, 0, 2)
+
+
 def solution(mesh):
     in_specs = (P("rep", "col", "row", None),)
     out_specs = P(("rep", "col"), "row", None)
-    return jax.shard_map(body, mesh=mesh, in_specs=in_specs, out_specs=out_specs, check_vma=False)
+    ways = mesh.shape["rep"] * mesh.shape["col"]
+    split_lines = (NB // mesh.shape["row"]) % ways == 0 and NA % (8 * ways) == 0
+    chosen = line_body if split_lines else body
+    return jax.shard_map(chosen, mesh=mesh, in_specs=in_specs, out_specs=out_specs, check_vma=False)

time: 1190 us -> 413 us (0.35)
  local copies, waits for them, and re-layouts: 451 us -> 36 us
  matrix products: 251 us -> 0 us
  other arithmetic: 237 us -> 5.56 us
  blocking collectives: 0 us -> 209 us
  waiting for transfers between devices: 188 us -> 94.8 us
  Pallas kernels: 0 us -> 49.8 us
  starting transfers between devices: 39.5 us -> 3.7 us
    dot_general x28 -> x0, matrix products: 251 us -> none  [the longest x18 134 us: matmul_high(): jnp.dot(first_matrix, second_matrix, precision=highest, preferred_element...]
    all_to_all x6 -> x0, other arithmetic: 227 us -> none  [the longest x1 40.4 us: body(): lax.all_to_all(imag_lines, ('rep', 'col'), split_axis=0, concat_axis=2, t...]
    all_to_all x0 -> x3, blocking collectives: none -> 209 us  [the longest x1 107 us: line_body(): lax.all_to_all(field, ('rep', 'col'), split_axis=1, concat_axis=0, tiled=...]
    all_to_all x8 -> x1, waiting for transfers between devices: 158 us -> 15.7 us  [carries(): ends = lax.all_to_all(ends, ('rep', 'col'), split_axis=1, concat_axis=1)]
    unnamed x66 -> x11, local copies, waits for them, and re-layouts: 135 us -> 15.6 us
    reshape x14 -> x0, local copies, waits for them, and re-layouts: 103 us -> none  [the longest x1 10.4 us: body(): flat_imag_in = imag_in.reshape(a_count * count, spec_len)]
    all_to_all x9 -> x3, local copies, waits for them, and re-layouts: 84.1 us -> 5.89 us  [the longest x1 3.65 us: line_body(): lines = lax.all_to_all(mine, 'col', split_axis=0, concat_axis=1, tiled=True)]
    scatter x6 -> x0, local copies, waits for them, and re-layouts: 67.4 us -> none  [the longest x1 24 us: body(): real_first.at[:, 0, :].set(jnp.where(owner_zero, new_r, packed_r))]
  transfers between devices with their start and end apart: 9 -> 3, of which waited for: 8 -> 3; matrix products, arithmetic and copies ran while one was open for 32% -> 0% of each run, Pallas kernels for 0% -> 0%
where the time goes in v1:
time: 413 us; the launch traced here: 412 us
  blocking collectives  209 us (51%)
  waiting for transfers between devices  94.8 us (23%)
  Pallas kernels  49.8 us (12%)
  local copies, waits for them, and re-layouts  36 us (9%)
  between operations  13.6 us (3%)
  other arithmetic  5.56 us (1%)
    all_to_all x1, blocking collectives, line_body(): lax.all_to_all(field, ('rep', 'col'), split_axis=1, concat_axis=0, tiled=...  107 us
    all_to_all x1, blocking collectives, line_body(): lines = lax.all_to_all(mine, 'col', split_axis=0, concat_axis=1, tiled=True)  83.5 us
    all_gather x1, waiting for transfers between devices, carries(): every = lax.all_gather(jnp.stack([total_up, total_down]), 'row', axis=0)  52 us
    reduce_scatter x1, waiting for transfers between devices, line_body(): mine = lax.psum_scatter(by_line, 'rep', scatter_dimension=0, tiled=True)  27.1 us
    pallas_call x1, Pallas kernels, backward_call(): pl.pallas_call(functools.partial(backward_kernel, scale), grid=(count,),...  25 us
    pallas_call x1, Pallas kernels, forward_call(): pl.pallas_call(forward_kernel, grid=(count,), in_specs=[whole(t.shape) fo...  24.8 us
    all_to_all x1, blocking collectives, carries(): back = lax.all_to_all(back, ('rep', 'col'), split_axis=1, concat_axis=1)  18.4 us
    all_to_all x1, waiting for transfers between devices, carries(): ends = lax.all_to_all(ends, ('rep', 'col'), split_axis=1, concat_axis=1)  15.7 us
  transfers between devices with their start and end apart: 3, of which 3 were waited for; matrix products, arithmetic and copies ran while one was open for 0% of the time, Pallas kernels for 0%

profile of v1, /device:TPU:0, one launch (start us, length us, event | category | flops | bytes accessed | tf_op | source)
XLA Modules:
  0.0 412.4 jit_solution(4365898291628258499)
XLA Ops:
  6.5 14.6 %copy.55 = f32[1,192,48,384]{3,1,2,0:T(8,128)} copy(f32[1,192,48,384]{3,2,1,0:T(8,128)} %param.7) | data formatting | bytes 28311552 | tf_op args[0]
  21.2 27.1 %reduce-scatter.2.cloned.1.call-done = f32[24,192,384]{2,1,0:T(8,128)} async-done(((f32[48,192,384]{2,1,0:T(8,128)}), f32[24,192,384]{2,1,0:T(8,128)}) %reduce-scatter.2.cloned.1.call-update) | async-done | bytes 7077904 | tf_op jit(solution)/shard_map/reduce_scatter | solution.py:397
  48.2 83.5 %all_to_all.46 = f32[24,192,384]{2,1,0:T(8,128)S(1)} all-to-all(f32[24,192,384]{2,1,0:T(8,128)} %reduce-scatter.2.cloned.1.call-done), channel_id=1, replica_groups=mesh['rep'=2,'row'=8,'col'=2] {'col'}, dimensions={0} | all-to-all | bytes 14155776 | tf_op jit(solution)/shard_map/all_to_all | solution.py:398
  131.7 3.6 copy.30
  135.4 24.8 %shard_map.73 = (f32[12,384,384]{2,1,0:T(8,128)}, f32[384,384]{1,0:T(8,128)}, f32[384,384]{1,0:T(8,128)}) custom-call(bf16[384,384]{1,0:T(8,128)(2,1)} %constant.138.clone.ah.ch, bf16[384,384]{1,0:T(8,128)(2,1)} %constant.139.clone.al.cl, bf16[384,384]{1,0:T(8,128)(2,1)} %constant.138.clone.ah.ch, bf16[384,384]{1,0:T(8,128)(2,1)} %constant.139.clone.al.cl, ...), custom_call_target="tpu_custom_call" | custom-call | tf_op jit(solution)/shard_map/pallas_call | solution.py:316
  160.2 2.3 pad_maximum_fusion
  162.6 3.7 all-to-all-start.1
  166.4 15.7 %all-to-all-done.1 = f32[2,4,96,384]{3,2,0,1:T(8,128)S(1)} async-done(((f32[2,4,96,384]{3,2,0,1:T(8,128)}), f32[2,4,96,384]{3,2,0,1:T(8,128)S(1)}, u32[]{:S(2)}, u32[]{:S(2)}) %all-to-all-start.1) | async-done | bytes 1179680 | tf_op jit(solution)/shard_map/all_to_all | solution.py:355
  182.0 0.2 fusion.37
  182.3 0.7 pad_maximum_fusion.2
  183.1 52.0 %all-gather.3.cloned.1.call-done = f32[16,96,384]{2,1,0:T(8,128)} async-done(((f32[2,96,384]{2,1,0:T(8,128)}), f32[16,96,384]{2,1,0:T(8,128)}) %all-gather.3.cloned.1.call-update) | async-done | bytes 2359312 | tf_op jit(solution)/shard_map/all_gather | solution.py:365
  235.2 2.1 multiply_add_fusion.3
  237.3 0.1 maximum_bitcast_fusion
  237.4 0.1 pad_maximum_fusion.1
  237.5 0.1 copy.40
  237.6 18.4 %all_to_all.47 = f32[2,4,96,384]{3,2,0,1:T(8,128)S(1)} all-to-all(f32[2,4,96,384]{3,2,0,1:T(8,128)S(1)} %copy.40), channel_id=1, replica_groups=mesh['rep'=2,'row'=8,'col'=2] {'rep','col'}, dimensions={1} | all-to-all | bytes 2359296 | tf_op jit(solution)/shard_map/all_to_all | solution.py:382
  255.9 0.1 copy.41
  256.0 0.9 copy-done
  256.9 0.1 copy-done.1
  257.0 25.0 %shard_map.74 = f32[12,384,384]{2,1,0:T(8,128)} custom-call(bf16[384,384]{1,0:T(8,128)(2,1)S(1)} %copy-done, bf16[384,384]{1,0:T(8,128)(2,1)S(1)} %copy-done.1, bf16[384,384]{1,0:T(8,128)(2,1)S(1)} %copy-done, bf16[384,384]{1,0:T(8,128)(2,1)S(1)} %copy-done.1, f32[384,1]{1,0:T(8,128)S(1)} %copy-done.2, f32[1,384]{1,0:T(1,128)S(1)} %copy-done.3, ...), custom_call_target="tpu_custom_call" | custom-call | tf_op jit(solution)/shard_map/pallas_call | solution.py:333
  282.0 7.3 %copy.42 = f32[12,384,384]{2,0,1:T(8,128)S(1)} copy(f32[12,384,384]{2,1,0:T(8,128)} %shard_map.74) | data formatting | bytes 14155776 | tf_op jit(solution)/shard_map/pallas_call | solution.py:333
  289.3 107.1 %all_to_all.48 = f32[12,384,384]{2,0,1:T(8,128)S(1)} all-to-all(f32[12,384,384]{2,0,1:T(8,128)S(1)} %copy.42), channel_id=1, replica_groups=mesh['rep'=2,'row'=8,'col'=2] {'rep','col'}, dimensions={1} | all-to-all | bytes 14155776 | tf_op jit(solution)/shard_map/all_to_all | solution.py:414
  396.4 2.2 copy.44
  398.5 7.1 %copy.45 = f32[96,48,384]{2,1,0:T(8,128)} copy(f32[96,48,384]{2,0,1:T(8,128)S(1)} %bitcast.230) | data formatting | bytes 14155776 | tf_op jit(solution)/shard_map/transpose | solution.py:415
  (13 shorter events, 0.2 us)
Async XLA Ops:
  6.5 41.7 %reduce-scatter.2.cloned.1.call-start = ((), (), s32[]{:S(2)}) async-start(), calls=%async_computation.5 | async-start | bytes 21233664 | tf_op jit(solution)/shard_map/reduce_scatter | solution.py:397
  162.6 3.7 copy-start.4
  162.6 19.5 %all-to-all-start.1 = ((f32[2,4,96,384]{3,2,0,1:T(8,128)}), f32[2,4,96,384]{3,2,0,1:T(8,128)S(1)}, u32[]{:S(2)}, u32[]{:S(2)}) async-start(f32[2,4,96,384]{3,2,0,1:T(8,128)} %pad_maximum_fusion), calls=%async_computation.2 | async-start | bytes 2359296 | tf_op jit(solution)/shard_map/all_to_all | solution.py:355
  166.2 68.9 %all-gather.3.cloned.1.call-start = ((), (), s32[]{:S(2)}) async-start(), calls=%async_computation.6 | async-start | bytes 2654208 | tf_op jit(solution)/shard_map/all_gather | solution.py:365
  255.9 1.0 copy-start
  255.9 1.0 copy-start.1
  255.9 1.1 copy-start.2
  255.9 1.1 copy-start.3
Sparse Core Ops, SparseCore 0:
  21.3 26.9 reduce-scatter.1
  183.1 51.9 all-gather.2

commit v2 on v1

--- a/solution.py
+++ b/solution.py
@@ -15,6 +15,10 @@
 
 
 highest = lax.Precision.HIGHEST
+MESH = pl.DeviceIdType.MESH
+GROUP = 8
+LANES = 128
+VMEM_BYTES = 56 * 1024 * 1024
 
 
 def wave_tables(freq_index, position, length):
@@ -261,84 +265,254 @@
     return 2.0 / (2.0 + shift + root), root
 
 
-def forward_kernel(ah, al, ch, cl, eig_a, eig_c, x_ref, z_ref, up_ref, down_ref, rho, power):
-    step = pl.program_id(0)
-    lines = times_table(x_ref[0], ch[...], cl[...])
-    modes = table_times(ah[...], al[...], lines)
-    z_ref[0] = modes
-
-    @pl.when(step == 0)
-    def _():
-        rho[...] = decay_of(eig_a[...] + eig_c[...] + 0.001)[0]
-        power[...] = rho[...]
-        up_ref[...] = modes
-        down_ref[...] = modes
-
-    @pl.when(step > 0)
-    def _():
+def peer_signal(semaphore, rep, col):
+    pl.semaphore_signal(
+        semaphore, inc=1, device_id={"rep": rep, "col": col}, device_id_type=MESH
+    )
+
+
+def send(source, target, send_sem, recv_sem, rep, col):
+    return pltpu.make_async_remote_copy(
+        src_ref=source,
+        dst_ref=target,
+        send_sem=send_sem,
+        recv_sem=recv_sem,
+        device_id={"rep": rep, "col": col},
+        device_id_type=MESH,
+    )
+
+
+def forward_kernel(
+    ah, al, ch, cl, eig_a, eig_c, x_ref,
+    z_ref, up_ref, down_ref,
+    own, other, sums, far, lines, rho, power,
+    own_sem, rep_send, rep_recv, col_send, col_recv,
+):
+    rep = lax.axis_index("rep")
+    col = lax.axis_index("col")
+    groups, bands, tall, band = own.shape
+    slab = tall // GROUP
+    count = z_ref.shape[0]
+    half = groups * GROUP
+
+    barrier = pltpu.get_barrier_semaphore()
+    peer_signal(barrier, 1 - rep, col)
+    peer_signal(barrier, rep, 1 - col)
+    pl.semaphore_wait(barrier, 2)
+
+    def place(n):
+        return (n + 1 - col) % groups
+
+    def rep_copy(n, j):
+        start = pl.multiple_of((1 - rep) * half + place(n) * GROUP, GROUP)
+        return send(
+            x_ref.at[:, pl.ds(start, GROUP), pl.ds(j * band, band)],
+            other.at[place(n), j].reshape(slab, GROUP, band),
+            rep_send.at[n, j],
+            rep_recv.at[n, j],
+            1 - rep,
+            col,
+        )
+
+    def own_copy(n, j):
+        start = pl.multiple_of(rep * half + place(n) * GROUP, GROUP)
+        return pltpu.make_async_copy(
+            x_ref.at[:, pl.ds(start, GROUP), pl.ds(j * band, band)],
+            own.at[place(n), j].reshape(slab, GROUP, band),
+            own_sem.at[n, j],
+        )
+
+    def col_copy(t):
+        return send(
+            sums.at[(1 - col) * count + t],
+            far.at[t],
+            col_send.at[t],
+            col_recv.at[t],
+            rep,
+            1 - col,
+        )
+
+    for n in range(groups):
+        for j in range(bands):
+            rep_copy(n, j).start()
+            own_copy(n, j).start()
+    decay, _ = decay_of(eig_a[...] + eig_c[...] + 0.001)
+    rho[...] = decay
+    power[...] = jnp.ones_like(decay)
+    up_ref[...] = jnp.zeros_like(decay)
+    down_ref[...] = jnp.zeros_like(decay)
+
+    for n in range(groups):
+        for j in range(bands):
+            rep_copy(n, j).wait_recv()
+            own_copy(n, j).wait()
+
+        def add(s, _):
+            line = place(n) * GROUP + s
+            rows = pl.ds(s, slab, stride=GROUP)
+            for j in range(bands):
+                sums[line, :, j * band : (j + 1) * band] = (
+                    own[place(n), j, rows, :] + other[place(n), j, rows, :]
+                )
+            t = line - (1 - col) * count
+
+            @pl.when((t >= 0) & (t < count))
+            def _():
+                col_copy(t).start()
+
+            return 0
+
+        lax.fori_loop(0, GROUP, add, 0)
+
+    def transform(t, _):
+        here = pl.ds(pl.multiple_of(col * slab, 8), slab)
+        there = pl.ds(pl.multiple_of((1 - col) * slab, 8), slab)
+        lines[here, :] = times_table(sums[col * count + t], ch[...], cl[...])
+        col_copy(t).wait_recv()
+        lines[there, :] = times_table(far[t], ch[...], cl[...])
+        modes = table_times(ah[...], al[...], lines[...])
+        z_ref[t] = modes
         up_ref[...] = modes + rho[...] * up_ref[...]
         down_ref[...] = down_ref[...] + power[...] * modes
         power[...] = power[...] * rho[...]
-
-
-def backward_kernel(scale, ah, al, ch, cl, eig_a, eig_c, z_ref, carry, out_ref, rho, gain, run, back):
-    step = pl.program_id(0)
+        return 0
+
+    lax.fori_loop(0, count, transform, 0)
+    for n in range(groups):
+        for j in range(bands):
+            rep_copy(n, j).wait_send()
+
+    def drain(t, _):
+        col_copy(t).wait_send()
+        return 0
+
+    lax.fori_loop(0, count, drain, 0)
+
+
+def backward_kernel(
+    scale,
+    ah, al, ch, cl, eig_a, eig_c, z_ref, carry,
+    out_ref,
+    rho, gain, run, back, planes,
+    own_sem, send_sem, recv_sem,
+):
+    rep = lax.axis_index("rep")
+    col = lax.axis_index("col")
     count = z_ref.shape[0]
-
-    @pl.when(step == 0)
-    def _():
-        decay, root = decay_of(eig_a[...] + eig_c[...] + 0.001)
-        rho[...] = decay
-        gain[...] = scale / root
-        run[...] = carry[0]
-        back[count - 1] = decay * carry[1]
-
-        def down(t, _):
-            here = count - 2 - t
-            back[here] = rho[...] * (z_ref[here + 1] + back[here + 1])
-            return 0
-
-        lax.fori_loop(0, count - 1, down, 0)
-
-    run[...] = z_ref[step] + rho[...] * run[...]
-    field = gain[...] * (run[...] + back[step])
-    lines = table_times(ah[...], al[...], field)
-    out_ref[0] = times_table(lines, ch[...], cl[...])
-
-
-def whole(shape):
-    return pl.BlockSpec(shape, lambda t: (0,) * len(shape))
+    slab = out_ref.shape[1]
+    offsets = ((0, 1), (1, 1), (1, 0))
+
+    barrier = pltpu.get_barrier_semaphore()
+    for flip_rep, flip_col in offsets:
+        peer_signal(barrier, (rep + flip_rep) % 2, (col + flip_col) % 2)
+    pl.semaphore_wait(barrier, 3)
+
+    mine = rep * 2 + col
+
+    def peer_copy(k, t):
+        to_rep = (rep + offsets[k][0]) % 2
+        to_col = (col + offsets[k][1]) % 2
+        start = pl.multiple_of((to_rep * 2 + to_col) * slab, 8)
+        return send(
+            planes.at[t, pl.ds(start, slab), :],
+            out_ref.at[mine * count + t],
+            send_sem.at[k, t],
+            recv_sem.at[k, t],
+            to_rep,
+            to_col,
+        )
+
+    def own_copy(t):
+        start = pl.multiple_of(mine * slab, 8)
+        return pltpu.make_async_copy(
+            planes.at[t, pl.ds(start, slab), :], out_ref.at[mine * count + t], own_sem.at[t]
+        )
+
+    decay, root = decay_of(eig_a[...] + eig_c[...] + 0.001)
+    rho[...] = decay
+    gain[...] = scale / root
+    run[...] = carry[0]
+    back[count - 1] = decay * carry[1]
+
+    def down(t, _):
+        here = count - 2 - t
+        back[here] = rho[...] * (z_ref[here + 1] + back[here + 1])
+        return 0
+
+    lax.fori_loop(0, count - 1, down, 0)
+
+    def emit(t, _):
+        run[...] = z_ref[t] + rho[...] * run[...]
+        field = gain[...] * (run[...] + back[t])
+        lines = table_times(ah[...], al[...], field)
+        planes[t] = times_table(lines, ch[...], cl[...])
+        for k in range(3):
+            peer_copy(k, t).start()
+        own_copy(t).start()
+        return 0
+
+    lax.fori_loop(0, count, emit, 0)
+
+    def drain(t, _):
+        own_copy(t).wait()
+        for k in range(3):
+            peer_copy(k, t).wait()
+        return 0
+
+    lax.fori_loop(0, count, drain, 0)
 
 
 def forward_call(x, tables):
-    count, rows, cols = x.shape
+    slab, width, cols = x.shape
+    rows = slab * 2
+    half = width // 2
+    count = half // 2
     plane = jax.ShapeDtypeStruct((rows, cols), jnp.float32)
+    modes = jax.ShapeDtypeStruct((count, rows, cols), jnp.float32)
+    vmem = pl.BlockSpec(memory_space=pltpu.VMEM)
+    groups = half // GROUP
+    dma = pltpu.SemaphoreType.DMA
+    f32 = jnp.float32
     return pl.pallas_call(
         forward_kernel,
-        grid=(count,),
-        in_specs=[whole(t.shape) for t in tables]
-        + [pl.BlockSpec((1, rows, cols), lambda t: (t, 0, 0))],
-        out_specs=[
-            pl.BlockSpec((1, rows, cols), lambda t: (t, 0, 0)),
-            whole((rows, cols)),
-            whole((rows, cols)),
+        in_specs=[vmem] * len(tables) + [pl.BlockSpec(memory_space=pl.ANY)],
+        out_specs=[vmem] * 3,
+        out_shape=[modes, plane, plane],
+        scratch_shapes=[
+            pltpu.VMEM((groups, cols // LANES, slab * GROUP, LANES), f32),
+            pltpu.VMEM((groups, cols // LANES, slab * GROUP, LANES), f32),
+            pltpu.VMEM((half, slab, cols), f32),
+            pltpu.VMEM((count, slab, cols), f32),
+            pltpu.VMEM((rows, cols), f32),
+            pltpu.VMEM((rows, cols), f32),
+            pltpu.VMEM((rows, cols), f32),
+            dma((groups, cols // LANES)),
+            dma((groups, cols // LANES)),
+            dma((groups, cols // LANES)),
+            dma((count,)),
+            dma((count,)),
         ],
-        out_shape=[jax.ShapeDtypeStruct(x.shape, jnp.float32), plane, plane],
-        scratch_shapes=[pltpu.VMEM((rows, cols), jnp.float32)] * 2,
+        compiler_params=pltpu.CompilerParams(
+            collective_id=0, has_side_effects=True, vmem_limit_bytes=VMEM_BYTES
+        ),
     )(*tables, x)
 
 
 def backward_call(z, carry, tables, scale):
     count, rows, cols = z.shape
+    vmem = pl.BlockSpec(memory_space=pltpu.VMEM)
+    dma = pltpu.SemaphoreType.DMA
     return pl.pallas_call(
         functools.partial(backward_kernel, scale),
-        grid=(count,),
-        in_specs=[whole(t.shape) for t in tables] + [whole(z.shape), whole(carry.shape)],
-        out_specs=pl.BlockSpec((1, rows, cols), lambda t: (t, 0, 0)),
-        out_shape=jax.ShapeDtypeStruct(z.shape, jnp.float32),
+        in_specs=[vmem] * (len(tables) + 2),
+        out_specs=pl.BlockSpec(memory_space=pl.ANY),
+        out_shape=jax.ShapeDtypeStruct((count * 4, rows // 4, cols), jnp.float32),
         scratch_shapes=[pltpu.VMEM((rows, cols), jnp.float32)] * 3
-        + [pltpu.VMEM(z.shape, jnp.float32)],
-        compiler_params=pltpu.CompilerParams(vmem_limit_bytes=50 * 1024 * 1024),
+        + [pltpu.VMEM(z.shape, jnp.float32)] * 2
+        + [dma((count,)), dma((3, count)), dma((3, count))],
+        compiler_params=pltpu.CompilerParams(
+            collective_id=1, has_side_effects=True, vmem_limit_bytes=VMEM_BYTES
+        ),
     )(*tables, z, carry)
 
 
@@ -385,17 +559,8 @@
 
 def line_body(sources):
     partial_value = sources[0]
-    rep_count = lax.axis_size("rep")
-    col_count = lax.axis_size("col")
     slab, width, length_c = partial_value.shape
-    length_a = slab * col_count
-    length_b = width * lax.axis_size("row")
-    half = width // rep_count
-    rep = lax.axis_index("rep")
-    part = half // col_count
-    by_line = partial_value.transpose(1, 0, 2)
-    mine = lax.psum_scatter(by_line, "rep", scatter_dimension=0, tiled=True)
-    lines = lax.all_to_all(mine, "col", split_axis=0, concat_axis=1, tiled=True)
+    length_a = slab * lax.axis_size("col")
     high_a, low_a = slab_tables(length_a)
     high_c, low_c = slab_tables(length_c)
     eig_a = eigen_values(length_a)
@@ -408,17 +573,16 @@
         jnp.asarray(eig_a)[:, None],
         jnp.asarray(eig_c)[None, :],
     )
-    modes, up, down = forward_call(lines, tables)
-    carry = carries(up, down, part, eig_a, eig_c)
-    field = backward_call(modes, carry, tables, 1.0 / (length_a * length_c))
-    result = lax.all_to_all(field, ("rep", "col"), split_axis=1, concat_axis=0, tiled=True)
+    modes, up, down = forward_call(partial_value, tables)
+    carry = carries(up, down, modes.shape[0], eig_a, eig_c)
+    result = backward_call(modes, carry, tables, 1.0 / (length_a * length_c))
     return result.transpose(1, 0, 2)
 
 
 def solution(mesh):
     in_specs = (P("rep", "col", "row", None),)
     out_specs = P(("rep", "col"), "row", None)
-    ways = mesh.shape["rep"] * mesh.shape["col"]
-    split_lines = (NB // mesh.shape["row"]) % ways == 0 and NA % (8 * ways) == 0
+    pairs = mesh.shape["rep"] == 2 and mesh.shape["col"] == 2
+    split_lines = pairs and (NB // mesh.shape["row"]) % (2 * GROUP) == 0 and NA % 32 == 0 and NC % LANES == 0
     chosen = line_body if split_lines else body
     return jax.shard_map(chosen, mesh=mesh, in_specs=in_specs, out_specs=out_specs, check_vma=False)

time: 413 us -> 299 us (0.72)
  blocking collectives: 209 us -> 18.4 us
  Pallas kernels: 49.8 us -> 177 us
  waiting for transfers between devices: 94.8 us -> 68.3 us
  local copies, waits for them, and re-layouts: 36 us -> 11.3 us
    all_to_all x2 -> x0, blocking collectives: 191 us -> none  [the longest x1 107 us: line_body(): lax.all_to_all(field, ('rep', 'col'), split_axis=1, concat_axis=0, tiled=...]
    pallas_call x2, Pallas kernels: 49.8 us -> 177 us  [the longest x1 91.1 us: forward_call(): pl.pallas_call(forward_kernel, in_specs=[vmem] * len(tables) + [pl.BlockS...]
    reduce_scatter x1 -> x0, waiting for transfers between devices: 27.1 us -> none  [line_body(): mine = lax.psum_scatter(by_line, 'rep', scatter_dimension=0, tiled=True)]
    unnamed x11 -> x2, local copies, waits for them, and re-layouts: 15.6 us -> 0.01 us
    pallas_call x1 -> x0, local copies, waits for them, and re-layouts: 7.25 us -> none  [backward_call(): pl.pallas_call(functools.partial(backward_kernel, scale), grid=(count,),...]
    all_to_all x2 -> x0, local copies, waits for them, and re-layouts: 5.81 us -> none  [the longest x1 3.65 us: line_body(): lines = lax.all_to_all(mine, 'col', split_axis=0, concat_axis=1, tiled=True)]
  transfers between devices with their start and end apart: 3 -> 2, of which waited for: 3 -> 2; matrix products, arithmetic and copies ran while one was open for 0% -> 0% of each run, Pallas kernels for 0% -> 0%
where the time goes in v2:
time: 299 us; the launch traced here: 298 us
  Pallas kernels  177 us (59%)
  waiting for transfers between devices  68.3 us (23%)
  blocking collectives  18.4 us (6%)
  between operations  13.6 us (5%)
  local copies, waits for them, and re-layouts  11.3 us (4%)
  other arithmetic  5.56 us (2%)
  starting transfers between devices  3.7 us (1%)
    pallas_call x1, Pallas kernels, forward_call(): pl.pallas_call(forward_kernel, in_specs=[vmem] * len(tables) + [pl.BlockS...  91.1 us
    pallas_call x1, Pallas kernels, backward_call(): pl.pallas_call(functools.partial(backward_kernel, scale), in_specs=[vmem]...  86.3 us
    all_gather x1, waiting for transfers between devices, carries(): every = lax.all_gather(jnp.stack([total_up, total_down]), 'row', axis=0)  52.6 us
    all_to_all x1, blocking collectives, carries(): back = lax.all_to_all(back, ('rep', 'col'), split_axis=1, concat_axis=1)  18.4 us
    all_to_all x1, waiting for transfers between devices, carries(): ends = lax.all_to_all(ends, ('rep', 'col'), split_axis=1, concat_axis=1)  15.8 us
    transpose x1, local copies, waits for them, and re-layouts, line_body(): return result.transpose(1, 0, 2)  10.1 us
  transfers between devices with their start and end apart: 2, of which 2 were waited for; matrix products, arithmetic and copies ran while one was open for 0% of the time, Pallas kernels for 0%

profile of v2, /device:TPU:0, one launch (start us, length us, event | category | flops | bytes accessed | tf_op | source)
XLA Modules:
  0.0 298.2 jit_solution(17434178578597263571)
XLA Ops:
  6.5 91.1 %shard_map.73 = (f32[12,384,384]{2,1,0:T(8,128)}, f32[384,384]{1,0:T(8,128)}, f32[384,384]{1,0:T(8,128)}) custom-call(bf16[384,384]{1,0:T(8,128)(2,1)} %constant.138.clone.ah.ch, bf16[384,384]{1,0:T(8,128)(2,1)} %constant.139.clone.al.cl, bf16[384,384]{1,0:T(8,128)(2,1)} %constant.138.clone.ah.ch, bf16[384,384]{1,0:T(8,128)(2,1)} %constant.139.clone.al.cl, ...), custom_call_target="tpu_custom_call" | custom-call | tf_op jit(solution)/shard_map/pallas_call | solution.py:476
  97.6 2.3 pad_maximum_fusion
  100.0 0.0 copy-start
  100.0 3.7 %all-to-all-start = ((f32[2,4,96,384]{3,2,0,1:T(8,128)}), f32[2,4,96,384]{3,2,0,1:T(8,128)S(1)}, u32[]{:S(2)}, u32[]{:S(2)}) async-start(f32[2,4,96,384]{3,2,0,1:T(8,128)} %pad_maximum_fusion), calls=%async_computation | async-start | bytes 2359296 | tf_op jit(solution)/shard_map/all_to_all | solution.py:529
  103.6 0.0 all-gather.3.cloned.1.call-start
  103.7 0.0 copy-done
  103.7 0.1 dynamic_slice.36
  103.8 15.8 %all-to-all-done = f32[2,4,96,384]{3,2,0,1:T(8,128)S(1)} async-done(((f32[2,4,96,384]{3,2,0,1:T(8,128)}), f32[2,4,96,384]{3,2,0,1:T(8,128)S(1)}, u32[]{:S(2)}, u32[]{:S(2)}) %all-to-all-start) | async-done | bytes 1179680 | tf_op jit(solution)/shard_map/all_to_all | solution.py:529
  119.5 0.2 fusion.37
  119.8 0.7 pad_maximum_fusion.2
  120.5 0.0 all-gather.3.cloned.1.call-update
  120.6 52.6 %all-gather.3.cloned.1.call-done = f32[16,96,384]{2,1,0:T(8,128)} async-done(((f32[2,96,384]{2,1,0:T(8,128)}), f32[16,96,384]{2,1,0:T(8,128)}) %all-gather.3.cloned.1.call-update) | async-done | bytes 2359312 | tf_op jit(solution)/shard_map/all_gather | solution.py:539
  173.2 2.1 multiply_add_fusion.3
  175.3 0.1 maximum_bitcast_fusion
  175.4 0.1 pad_maximum_fusion.1
  175.5 0.1 copy.18
  175.5 18.4 %all_to_all.10 = f32[2,4,96,384]{3,2,0,1:T(8,128)S(1)} all-to-all(f32[2,4,96,384]{3,2,0,1:T(8,128)S(1)} %copy.18), channel_id=1, replica_groups=mesh['rep'=2,'row'=8,'col'=2] {'rep','col'}, dimensions={1} | all-to-all | bytes 2359296 | tf_op jit(solution)/shard_map/all_to_all | solution.py:556
  193.9 1.1 copy.19
  195.0 86.3 %shard_map.74 = f32[48,96,384]{2,1,0:T(8,128)} custom-call(bf16[384,384]{1,0:T(8,128)(2,1)} %constant.138.clone.ah.ch, bf16[384,384]{1,0:T(8,128)(2,1)} %constant.139.clone.al.cl, bf16[384,384]{1,0:T(8,128)(2,1)} %constant.138.clone.ah.ch, bf16[384,384]{1,0:T(8,128)(2,1)} %constant.139.clone.al.cl, f32[384,1]{1,0:T(8,128)} %constant.142.eig_a, ...), custom_call_target="tpu_custom_call" | custom-call | tf_op jit(solution)/shard_map/pallas_call | solution.py:505
  281.3 10.1 %copy.20 = f32[96,48,384]{2,1,0:T(8,128)} copy(f32[96,48,384]{2,0,1:T(8,128)} %bitcast.212) | data formatting | bytes 14155776 | tf_op jit(solution)/shard_map/transpose | solution.py:579
Async XLA Ops:
  100.0 3.7 %copy-start = (f32[384]{0:T(512)S(1)}, f32[384]{0:T(512)}, u32[]{:S(2)}) copy-start(f32[384]{0:T(512)} %constant.140.clone) | copy-start | bytes 4612
  100.0 19.6 %all-to-all-start = ((f32[2,4,96,384]{3,2,0,1:T(8,128)}), f32[2,4,96,384]{3,2,0,1:T(8,128)S(1)}, u32[]{:S(2)}, u32[]{:S(2)}) async-start(f32[2,4,96,384]{3,2,0,1:T(8,128)} %pad_maximum_fusion), calls=%async_computation | async-start | bytes 2359296 | tf_op jit(solution)/shard_map/all_to_all | solution.py:529
  103.6 69.6 %all-gather.3.cloned.1.call-start = ((), (), s32[]{:S(2)}) async-start(), calls=%async_computation.2 | async-start | bytes 2654208 | tf_op jit(solution)/shard_map/all_gather | solution.py:539
Sparse Core Ops, SparseCore 0:
  120.6 52.4 all-gather.2

commit v3 on v2

--- a/solution.py
+++ b/solution.py
@@ -265,71 +265,257 @@
     return 2.0 / (2.0 + shift + root), root
 
 
-def peer_signal(semaphore, rep, col):
-    pl.semaphore_signal(
-        semaphore, inc=1, device_id={"rep": rep, "col": col}, device_id_type=MESH
-    )
-
-
-def send(source, target, send_sem, recv_sem, rep, col):
+def peer_signal(semaphore, device):
+    pl.semaphore_signal(semaphore, inc=1, device_id=device, device_id_type=MESH)
+
+
+def send(source, target, send_sem, recv_sem, device):
     return pltpu.make_async_remote_copy(
         src_ref=source,
         dst_ref=target,
         send_sem=send_sem,
         recv_sem=recv_sem,
-        device_id={"rep": rep, "col": col},
+        device_id=device,
         device_id_type=MESH,
     )
+
+
+def power_of(base, exponent):
+    result = None
+    while exponent:
+        if exponent & 1:
+            result = base if result is None else result * base
+        base = base * base
+        exponent >>= 1
+    return result
+
+
+def exchange_carries(
+    depths, count, up_ref, down_ref, rho, carry,
+    e_in, f_out, f_in, g_out, g_in, h_out, h_in, c_out, c_in, x_out, x_in, y_in, r_out,
+    sends, recvs,
+):
+    rep = lax.axis_index("rep")
+    col = lax.axis_index("col")
+    row = lax.axis_index("row")
+    x = row % 2
+    z = row // 2
+    depth = depths
+    tall = depth * 8
+    chunk = tall * 4
+    chunks = up_ref.shape[0] // chunk
+    other_rep = {"rep": 1 - rep}
+    other_col = {"col": 1 - col}
+    other_x = {"row": z * 2 + 1 - x}
+    ends = (up_ref, down_ref)
+
+    def at_z(m):
+        return (z + m) % depth
+
+    def rows_of(q):
+        return pl.multiple_of(q * chunk + rep * (2 * tall), 8)
+
+    def theta(start, size, blocks):
+        return power_of(rho[pl.ds(start, size), :], count * blocks)
+
+    def copy(source, target, q, n, device):
+        return send(source, target, sends.at[q, n], recvs.at[q, n], device)
+
+    def rep_in(q):
+        start = pl.multiple_of(q * chunk + (1 - rep) * (2 * tall), 8)
+        return [
+            copy(ends[k].at[pl.ds(start, 2 * tall), :], e_in.at[q, k], q, k, other_rep)
+            for k in range(2)
+        ]
+
+    def col_in(q):
+        return [copy(f_out.at[q, col], f_in.at[q], q, 2, other_col)]
+
+    def x_send(q):
+        start = pl.multiple_of((1 - x) * tall, 8)
+        return [copy(g_out.at[q, pl.ds(start, tall), :], g_in.at[q], q, 3, other_x)]
+
+    def z_send(q):
+        return [
+            copy(
+                h_out.at[q, pl.ds(pl.multiple_of(at_z(m) * 8, 8), 8), :],
+                h_in.at[q, z],
+                q,
+                3 + m,
+                {"row": at_z(m) * 2 + x},
+            )
+            for m in range(1, depth)
+        ]
+
+    def z_back(q):
+        return [
+            copy(
+                c_out.at[q, at_z(m)],
+                c_in.at[q, pl.ds(pl.multiple_of(z * 8, 8), 8), :],
+                q,
+                2 + depth + m,
+                {"row": at_z(m) * 2 + x},
+            )
+            for m in range(1, depth)
+        ]
+
+    def x_back(q):
+        here = pl.ds(pl.multiple_of(x * tall, 8), tall)
+        return [copy(x_out.at[q], x_in.at[q, here, :], q, 2 + 2 * depth, other_x)]
+
+    def col_back(q):
+        return [copy(x_in.at[q], y_in.at[q], q, 3 + 2 * depth, other_col)]
+
+    def rep_back(q):
+        return [
+            copy(
+                r_out.at[q, k],
+                carry.at[k, pl.ds(rows_of(q), 2 * tall), :],
+                q,
+                4 + 2 * depth + k,
+                other_rep,
+            )
+            for k in range(2)
+        ]
+
+    def ends_of(q, k):
+        mine = ends[k][pl.ds(rows_of(q), 2 * tall), :]
+        theirs = e_in[q, k]
+        first = jnp.where(rep == 0, mine, theirs)
+        second = jnp.where(rep == 0, theirs, mine)
+        return first, second
+
+    def join_rep(q):
+        block = theta(rows_of(q), 2 * tall, 1)
+        first, second = ends_of(q, 0)
+        f_out[q, 0] = second + block * first
+        first, second = ends_of(q, 1)
+        f_out[q, 1] = first + block * second
+
+    def join_col(q):
+        g_out[q] = f_out[q, 1 - col] + theta(rows_of(q), 2 * tall, 2) * f_in[q]
+
+    def quarter(q):
+        return pl.multiple_of(rows_of(q) + x * tall, 8)
+
+    def mine_x(q):
+        return g_out[q, pl.ds(pl.multiple_of(x * tall, 8), tall), :]
+
+    def join_x(q):
+        near = jnp.where(x == col, mine_x(q), g_in[q])
+        away = jnp.where(x == col, g_in[q], mine_x(q))
+        h_out[q] = near + theta(quarter(q), tall, 4) * away
+        h_in[q, z] = h_out[q, pl.ds(pl.multiple_of(z * 8, 8), 8), :]
+
+    def join_z(q):
+        wide = theta(pl.multiple_of(quarter(q) + z * 8, 8), 8, 8)
+        closing = 1.0 / (1.0 - power_of(wide, depth))
+        step = 2 * col - 1
+        for target in range(depth):
+            total = h_in[q, target]
+            for m in range(depth - 1, 0, -1):
+                total = h_in[q, (target + depth - step * m) % depth] + wide * total
+            c_out[q, target] = total * closing
+        c_in[q, pl.ds(pl.multiple_of(z * 8, 8), 8), :] = c_out[q, z]
+
+    def split_x(q):
+        into = c_in[q]
+        away = jnp.where(x == col, g_in[q], mine_x(q))
+        later = away + theta(quarter(q), tall, 4) * into
+        x_in[q, pl.ds(pl.multiple_of(x * tall, 8), tall), :] = jnp.where(x == col, later, into)
+        x_out[q] = jnp.where(x == col, into, later)
+
+    def split_rep(q):
+        start = rows_of(q)
+        here = pl.ds(start, 2 * tall)
+        block = theta(start, 2 * tall, 1)
+        handled = f_in[q] + theta(start, 2 * tall, 2) * x_in[q]
+        into_up = jnp.where(col == 1, handled, y_in[q])
+        into_down = jnp.where(col == 1, y_in[q], handled)
+        later_up = ends_of(q, 0)[0] + block * into_up
+        later_down = ends_of(q, 1)[1] + block * into_down
+        carry[0, here, :] = jnp.where(rep == 0, into_up, later_up)
+        carry[1, here, :] = jnp.where(rep == 0, later_down, into_down)
+        r_out[q, 0] = jnp.where(rep == 0, later_up, into_up)
+        r_out[q, 1] = jnp.where(rep == 0, into_down, later_down)
+
+    def nothing(q):
+        return None
+
+    moves = (rep_in, col_in, x_send, z_send, z_back, x_back, col_back, rep_back)
+    works = (nothing, join_rep, join_col, join_x, join_z, split_x, nothing, split_rep, nothing)
+    for moment in range(chunks + len(moves)):
+        for q in range(chunks):
+            phase = moment - q
+            if phase < 0 or phase > len(moves):
+                continue
+            if phase > 0:
+                for item in moves[phase - 1](q):
+                    item.wait_recv()
+            works[phase](q)
+            if phase < len(moves):
+                for item in moves[phase](q):
+                    item.start()
+    for q in range(chunks):
+        for move in moves:
+            for item in move(q):
+                item.wait_send()
 
 
 def forward_kernel(
     ah, al, ch, cl, eig_a, eig_c, x_ref,
-    z_ref, up_ref, down_ref,
-    own, other, sums, far, lines, rho, power,
+    z_ref, carry_ref,
+    own, other, sums, far, lines, rho, power, up_ref, down_ref, carry,
     own_sem, rep_send, rep_recv, col_send, col_recv,
+    *ring,
 ):
+    row = lax.axis_index("row")
+    depth = lax.axis_size("row") // 2
     rep = lax.axis_index("rep")
     col = lax.axis_index("col")
     groups, bands, tall, band = own.shape
     slab = tall // GROUP
     count = z_ref.shape[0]
-    half = groups * GROUP
+    shift = GROUP // 2
 
     barrier = pltpu.get_barrier_semaphore()
-    peer_signal(barrier, 1 - rep, col)
-    peer_signal(barrier, rep, 1 - col)
-    pl.semaphore_wait(barrier, 2)
-
-    def place(n):
-        return (n + 1 - col) % groups
+    peer_signal(barrier, {"rep": 1 - rep})
+    peer_signal(barrier, {"col": 1 - col})
+    peer_signal(barrier, {"row": row + 1 - 2 * (row % 2)})
+    for m in range(1, depth):
+        peer_signal(barrier, {"row": (row // 2 + m) % depth * 2 + row % 2})
+    pl.semaphore_wait(barrier, 2 + depth)
+
+    def first_line(n, owner):
+        chain = 1 - col if n < 2 else col
+        start = chain * (2 * count) + (owner + n % 2) * GROUP
+        return pl.multiple_of(start, GROUP)
 
     def rep_copy(n, j):
-        start = pl.multiple_of((1 - rep) * half + place(n) * GROUP, GROUP)
+        start = first_line(n, 1 - rep)
         return send(
             x_ref.at[:, pl.ds(start, GROUP), pl.ds(j * band, band)],
-            other.at[place(n), j].reshape(slab, GROUP, band),
+            other.at[n, j].reshape(slab, GROUP, band),
             rep_send.at[n, j],
             rep_recv.at[n, j],
-            1 - rep,
-            col,
+            {"rep": 1 - rep},
         )
 
     def own_copy(n, j):
-        start = pl.multiple_of(rep * half + place(n) * GROUP, GROUP)
+        start = first_line(n, rep)
         return pltpu.make_async_copy(
             x_ref.at[:, pl.ds(start, GROUP), pl.ds(j * band, band)],
-            own.at[place(n), j].reshape(slab, GROUP, band),
+            own.at[n, j].reshape(slab, GROUP, band),
             own_sem.at[n, j],
         )
 
     def col_copy(t):
         return send(
-            sums.at[(1 - col) * count + t],
+            sums.at[0, t],
             far.at[t],
             col_send.at[t],
             col_recv.at[t],
-            rep,
-            1 - col,
+            {"col": 1 - col},
         )
 
     for n in range(groups):
@@ -348,17 +534,17 @@
             own_copy(n, j).wait()
 
         def add(s, _):
-            line = place(n) * GROUP + s
+            t = n % 2 * GROUP + s - shift * rep
             rows = pl.ds(s, slab, stride=GROUP)
-            for j in range(bands):
-                sums[line, :, j * band : (j + 1) * band] = (
-                    own[place(n), j, rows, :] + other[place(n), j, rows, :]
-                )
-            t = line - (1 - col) * count
 
             @pl.when((t >= 0) & (t < count))
             def _():
-                col_copy(t).start()
+                for j in range(bands):
+                    sums[n // 2, t, :, j * band : (j + 1) * band] = (
+                        own[n, j, rows, :] + other[n, j, rows, :]
+                    )
+                if n < 2:
+                    col_copy(t).start()
 
             return 0
 
@@ -367,7 +553,7 @@
     def transform(t, _):
         here = pl.ds(pl.multiple_of(col * slab, 8), slab)
         there = pl.ds(pl.multiple_of((1 - col) * slab, 8), slab)
-        lines[here, :] = times_table(sums[col * count + t], ch[...], cl[...])
+        lines[here, :] = times_table(sums[1, t], ch[...], cl[...])
         col_copy(t).wait_recv()
         lines[there, :] = times_table(far[t], ch[...], cl[...])
         modes = table_times(ah[...], al[...], lines[...])
@@ -378,6 +564,8 @@
         return 0
 
     lax.fori_loop(0, count, transform, 0)
+    exchange_carries(depth, count, up_ref, down_ref, rho, carry, *ring)
+    carry_ref[...] = carry[...]
     for n in range(groups):
         for j in range(bands):
             rep_copy(n, j).wait_send()
@@ -404,10 +592,11 @@
 
     barrier = pltpu.get_barrier_semaphore()
     for flip_rep, flip_col in offsets:
-        peer_signal(barrier, (rep + flip_rep) % 2, (col + flip_col) % 2)
+        peer_signal(barrier, {"rep": (rep + flip_rep) % 2, "col": (col + flip_col) % 2})
     pl.semaphore_wait(barrier, 3)
 
     mine = rep * 2 + col
+    block = col * 2 + rep
 
     def peer_copy(k, t):
         to_rep = (rep + offsets[k][0]) % 2
@@ -415,17 +604,16 @@
         start = pl.multiple_of((to_rep * 2 + to_col) * slab, 8)
         return send(
             planes.at[t, pl.ds(start, slab), :],
-            out_ref.at[mine * count + t],
+            out_ref.at[block * count + t],
             send_sem.at[k, t],
             recv_sem.at[k, t],
-            to_rep,
-            to_col,
+            {"rep": to_rep, "col": to_col},
         )
 
     def own_copy(t):
         start = pl.multiple_of(mine * slab, 8)
         return pltpu.make_async_copy(
-            planes.at[t, pl.ds(start, slab), :], out_ref.at[mine * count + t], own_sem.at[t]
+            planes.at[t, pl.ds(start, slab), :], out_ref.at[block * count + t], own_sem.at[t]
         )
 
     decay, root = decay_of(eig_a[...] + eig_c[...] + 0.001)
@@ -467,31 +655,44 @@
     rows = slab * 2
     half = width // 2
     count = half // 2
-    plane = jax.ShapeDtypeStruct((rows, cols), jnp.float32)
+    carry = jax.ShapeDtypeStruct((2, rows, cols), jnp.float32)
     modes = jax.ShapeDtypeStruct((count, rows, cols), jnp.float32)
     vmem = pl.BlockSpec(memory_space=pltpu.VMEM)
-    groups = half // GROUP
+    groups = 4
+    depth = lax.axis_size("row") // 2
+    tall = depth * 8
+    chunks = rows // (4 * tall)
     dma = pltpu.SemaphoreType.DMA
     f32 = jnp.float32
     return pl.pallas_call(
         forward_kernel,
         in_specs=[vmem] * len(tables) + [pl.BlockSpec(memory_space=pl.ANY)],
-        out_specs=[vmem] * 3,
-        out_shape=[modes, plane, plane],
+        out_specs=[vmem] * 2,
+        out_shape=[modes, carry],
         scratch_shapes=[
             pltpu.VMEM((groups, cols // LANES, slab * GROUP, LANES), f32),
             pltpu.VMEM((groups, cols // LANES, slab * GROUP, LANES), f32),
-            pltpu.VMEM((half, slab, cols), f32),
+            pltpu.VMEM((2, count, slab, cols), f32),
             pltpu.VMEM((count, slab, cols), f32),
-            pltpu.VMEM((rows, cols), f32),
-            pltpu.VMEM((rows, cols), f32),
-            pltpu.VMEM((rows, cols), f32),
+        ]
+        + [pltpu.VMEM((rows, cols), f32)] * 5
+        + [
+            pltpu.VMEM((2, rows, cols), f32),
             dma((groups, cols // LANES)),
             dma((groups, cols // LANES)),
             dma((groups, cols // LANES)),
             dma((count,)),
             dma((count,)),
-        ],
+        ]
+        + [
+            pltpu.VMEM((chunks,) + shape + (cols,), f32)
+            for shape in (
+                (2, 2 * tall), (2, 2 * tall), (2 * tall,), (2 * tall,), (tall,), (tall,),
+                (depth, 8), (depth, 8), (tall,), (tall,), (2 * tall,), (2 * tall,),
+                (2, 2 * tall),
+            )
+        ]
+        + [dma((chunks, 6 + 2 * depth))] * 2,
         compiler_params=pltpu.CompilerParams(
             collective_id=0, has_side_effects=True, vmem_limit_bytes=VMEM_BYTES
         ),
@@ -516,47 +717,6 @@
     )(*tables, z, carry)
 
 
-def carries(up, down, count, eig_a, eig_c):
-    rows, cols = up.shape
-    rep_count = lax.axis_size("rep")
-    col_count = lax.axis_size("col")
-    row_count = lax.axis_size("row")
-    group = rep_count * col_count
-    part = rows // group
-    member = lax.axis_index("rep") * col_count + lax.axis_index("col")
-    row = lax.axis_index("row")
-    ends = jnp.stack([up, down]).reshape(2, group, part, cols)
-    ends = lax.all_to_all(ends, ("rep", "col"), split_axis=1, concat_axis=1)
-    eig_part = lax.dynamic_slice_in_dim(jnp.asarray(eig_a), member * part, part, 0)
-    rho, _ = decay_of(eig_part[:, None] + jnp.asarray(eig_c)[None, :] + 0.001)
-    block = lax.integer_pow(rho, count)
-    wide = lax.integer_pow(block, group)
-    total_up = ends[0, 0]
-    total_down = ends[1, group - 1]
-    for j in range(1, group):
-        total_up = ends[0, j] + block * total_up
-        total_down = ends[1, group - 1 - j] + block * total_down
-    every = lax.all_gather(jnp.stack([total_up, total_down]), "row", axis=0)
-
-    def pick(offset, side):
-        return lax.dynamic_index_in_dim(every, (row + offset) % row_count, 0, False)[side]
-
-    into_up = pick(0, 0)
-    into_down = pick(0, 1)
-    for m in range(row_count - 1, 0, -1):
-        into_up = pick(row_count - m, 0) + wide * into_up
-        into_down = pick(m, 1) + wide * into_down
-    closing = 1.0 / (1.0 - lax.integer_pow(wide, row_count))
-    ups = [into_up * closing]
-    downs = [into_down * closing]
-    for j in range(group - 1):
-        ups.append(ends[0, j] + block * ups[-1])
-        downs.append(ends[1, group - 1 - j] + block * downs[-1])
-    back = jnp.stack([jnp.stack(ups), jnp.stack(downs[::-1])])
-    back = lax.all_to_all(back, ("rep", "col"), split_axis=1, concat_axis=1)
-    return back.reshape(2, rows, cols)
-
-
 def line_body(sources):
     partial_value = sources[0]
     slab, width, length_c = partial_value.shape
@@ -573,8 +733,7 @@
         jnp.asarray(eig_a)[:, None],
         jnp.asarray(eig_c)[None, :],
     )
-    modes, up, down = forward_call(partial_value, tables)
-    carry = carries(up, down, modes.shape[0], eig_a, eig_c)
+    modes, carry = forward_call(partial_value, tables)
     result = backward_call(modes, carry, tables, 1.0 / (length_a * length_c))
     return result.transpose(1, 0, 2)
 
@@ -583,6 +742,8 @@
     in_specs = (P("rep", "col", "row", None),)
     out_specs = P(("rep", "col"), "row", None)
     pairs = mesh.shape["rep"] == 2 and mesh.shape["col"] == 2
-    split_lines = pairs and (NB // mesh.shape["row"]) % (2 * GROUP) == 0 and NA % 32 == 0 and NC % LANES == 0
+    rows = mesh.shape["row"]
+    split_lines = pairs and rows % 2 == 0 and NB == rows * 6 * GROUP
+    split_lines = split_lines and NA % (16 * rows) == 0 and NC % LANES == 0
     chosen = line_body if split_lines else body
     return jax.shard_map(chosen, mesh=mesh, in_specs=in_specs, out_specs=out_specs, check_vma=False)

time: 299 us -> 224 us (0.75)
  waiting for transfers between devices: 68.3 us -> 0 us
  Pallas kernels: 177 us -> 214 us
  blocking collectives: 18.4 us -> 0 us
  between operations: 13.6 us -> 0.02 us
  other arithmetic: 5.56 us -> 0 us
  starting transfers between devices: 3.7 us -> 0 us
    all_gather x1 -> x0, waiting for transfers between devices: 52.6 us -> none  [carries(): every = lax.all_gather(jnp.stack([total_up, total_down]), 'row', axis=0)]
    pallas_call x1, Pallas kernels: 91.1 us -> 128 us  [forward_call(): pl.pallas_call(forward_kernel, in_specs=[vmem] * len(tables) + [pl.BlockS...]
    all_to_all x1 -> x0, blocking collectives: 18.4 us -> none  [carries(): back = lax.all_to_all(back, ('rep', 'col'), split_axis=1, concat_axis=1)]
    all_to_all x1 -> x0, waiting for transfers between devices: 15.8 us -> none  [carries(): ends = lax.all_to_all(ends, ('rep', 'col'), split_axis=1, concat_axis=1)]
    all_to_all x1 -> x0, starting transfers between devices: 3.66 us -> none  [carries(): ends = lax.all_to_all(ends, ('rep', 'col'), split_axis=1, concat_axis=1)]
    another operation x4 -> x0, other arithmetic: 3.24 us -> none  [the longest x1 2.35 us: carries(): ends = jnp.stack([up, down]).reshape(2, group, part, cols)]
  transfers between devices with their start and end apart: 2 -> 0, of which waited for: 2 -> 0; matrix products, arithmetic and copies ran while one was open for 0% -> 0% of each run, Pallas kernels for 0% -> 0%
where the time goes in v3:
time: 224 us
  Pallas kernels  214 us (96%)
  local copies, waits for them, and re-layouts  10.1 us (5%)
    pallas_call x1, Pallas kernels, forward_call(): pl.pallas_call(forward_kernel, in_specs=[vmem] * len(tables) + [pl.BlockS...  128 us
    pallas_call x1, Pallas kernels, backward_call(): pl.pallas_call(functools.partial(backward_kernel, scale), in_specs=[vmem]...  86.3 us
    transpose x1, local copies, waits for them, and re-layouts, line_body(): return result.transpose(1, 0, 2)  10.1 us

profile of v3, /device:TPU:0, one launch (start us, length us, event | category | flops | bytes accessed | tf_op | source)
XLA Modules:
  0.0 224.0 jit_solution(14994562057500714508)
XLA Ops:
  0.0 127.6 %shard_map.73 = (f32[12,384,384]{2,1,0:T(8,128)}, f32[2,384,384]{2,1,0:T(8,128)}) custom-call(bf16[384,384]{1,0:T(8,128)(2,1)} %constant.6.clone.ah.ch, bf16[384,384]{1,0:T(8,128)(2,1)} %constant.7.clone.al.cl, bf16[384,384]{1,0:T(8,128)(2,1)} %constant.6.clone.ah.ch, bf16[384,384]{1,0:T(8,128)(2,1)} %constant.7.clone.al.cl, f32[384,1]{1,0:T(8,128)} %constant.10.eig_a, ...), custom_call_target="tpu_custom_call" | custom-call | tf_op jit(solution)/shard_map/pallas_call | solution.py:667
  127.6 86.3 %shard_map.74 = f32[48,96,384]{2,1,0:T(8,128)} custom-call(bf16[384,384]{1,0:T(8,128)(2,1)} %constant.6.clone.ah.ch, bf16[384,384]{1,0:T(8,128)(2,1)} %constant.7.clone.al.cl, bf16[384,384]{1,0:T(8,128)(2,1)} %constant.6.clone.ah.ch, bf16[384,384]{1,0:T(8,128)(2,1)} %constant.7.clone.al.cl, f32[384,1]{1,0:T(8,128)} %constant.10.eig_a, ...), custom_call_target="tpu_custom_call" | custom-call | tf_op jit(solution)/shard_map/pallas_call | solution.py:706
  213.9 10.1 %copy.8 = f32[96,48,384]{2,1,0:T(8,128)} copy(f32[96,48,384]{2,0,1:T(8,128)} %bitcast.2) | data formatting | bytes 14155776 | tf_op jit(solution)/shard_map/transpose | solution.py:738
